TPU v7x, 32 devices: a 4x4x1 block of a 4x4x8 slice. The times are simulated.
32 devices in a mesh: batch: 1 (over z), cols: 4 (over y), rows: 8 (over x, core).
Axes of the slice: x: 4, y: 4, z: 1, core: 2. Of those that a mesh axis runs over, the one named last changes fastest.
The devices are a block of a 4x4x8 slice.
Arguments:
- frames: bfloat16 [24, 1, 384, 384, 16], P(None, 'batch', 'rows', 'cols')
- h_init: float32 [1, 384, 384, 64], P('batch', 'rows', 'cols')
- w_x: bfloat16 [3, 3, 16, 192], replicated
- w_hzr: bfloat16 [3, 3, 64, 128], replicated
- w_hn: bfloat16 [3, 3, 64, 64], replicated
- gate_bias: float32 [192], replicated
Outputs:
- output 1: bfloat16 [24, 1, 384, 384, 64], P(None, 'batch', 'rows', 'cols')
- output 2: float32 [1, 384, 384, 64], P('batch', 'rows', 'cols')
All inputs are finite; a program needn't handle non-finite values.
Results may differ from a plain program's by a relative error of at most 0.00441273.
Values are sent between devices in bfloat16 or wider.
A program may use at most 768 MiB of HBM per device.

v0:
```python
import functools

import jax
import jax.numpy as jnp
from jax import lax
from jax.experimental import pallas as pl
from jax.experimental.pallas import tpu as pltpu
from jax.sharding import PartitionSpec as P

MESH = pl.DeviceIdType.MESH
LANES = 128
BF = jnp.bfloat16
F32 = jnp.float32

ROW_STEPS = 2
HR = 2 * ROW_STEPS
HC = 8
COL_STEPS = HC // 2
VMEM_MIB = 22
PER = LANES // HC


def store3(buf, base, size, val):
    buf[pl.ds(base, size), :] = pltpu.roll(val, 1, 1)
    buf[pl.ds(base + size, size), :] = val
    buf[pl.ds(base + 2 * size, size), :] = pltpu.roll(val, LANES - 1, 1)


def spin(val, shift):
    shift = shift % LANES
    return pltpu.roll(val, shift, 1) if shift else val


def kernel(n_rows, n_cols, frames, h0, w_x, w_hzr, w_hn, bias, out, hlast,
           H, HB, RB, XB, Z, KM, WZR, WN, HI, FS, XF, FC, FR, CS, CR, DS, DR, RS, RR,
           hi_sem, fs_sem, fc_send, fc_recv, fh_send, fh_recv,
           cs_send, cs_recv, dg_send, dg_recv, rr_send, rr_recv):
    steps, tile_h, ch, tile_w = out.shape
    cin = frames.shape[2]
    total_rows = tile_h + 2 * HR
    n_slots = tile_w // HC
    n_groups = tile_h // PER
    n_supers = steps // COL_STEPS
    per_super = COL_STEPS // ROW_STEPS
    row = lax.axis_index('rows')
    col = lax.axis_index('cols')
    has_v = (row > 0, row < n_rows - 1)
    has_h = (col > 0, col < n_cols - 1)
    diag = [(v, h, jnp.logical_and(has_v[v], has_h[h])) for v in range(2) for h in range(2)]

    def v_dev(v):
        return {'rows': row + 2 * v - 1}

    def h_dev(h):
        return {'cols': col + 2 * h - 1}

    def remote(src, dst, send, recv, dev):
        return pltpu.make_async_remote_copy(src, dst, send, recv, device_id=dev, device_id_type=MESH)

    def when_do(cond, *fns):
        @pl.when(cond)
        def _():
            for fn in fns:
                fn()

    lane = lax.broadcasted_iota(jnp.int32, (ch, LANES), 1)
    slot_of = lane // HC
    lane_x = lax.broadcasted_iota(jnp.int32, (cin, LANES), 1)
    slot_x = lane_x // HC
    middle = (tile_w + HC + LANES - HC) // 2
    ones = jnp.where(lax.broadcasted_iota(jnp.int32, (64, LANES), 0) < 3, 1.0, 0.0).astype(BF)
    ok = [jnp.where(c, 1, 0) for c in has_v + has_h]
    lane_ok = jnp.where(lane < tile_w, 1, jnp.where(lane < tile_w + HC, ok[3], jnp.where(lane >= LANES - HC, ok[2], 0)))
    lead = n_slots - 1

    def pack_rows(rows, slots, dtype):
        acc = [jnp.zeros(rows[0].shape, dtype), jnp.zeros(rows[0].shape, dtype)]
        for q, val in enumerate(rows):
            here = jnp.logical_or(slots == q, slots == (lead + q) % PER)
            acc[q % 2] = jnp.where(here, spin(val, HC * q), acc[q % 2])
        even = slots % 2 == 0
        return jnp.where(even, acc[0], acc[1]), jnp.where(even, acc[1], acc[0])

    def halo_rows(from_left, from_right, slots):
        turned = spin(from_left, HC * (3 - lead))
        even = slots % 2 == 0
        mixed = (jnp.where(even, from_right, turned), jnp.where(even, turned, from_right))
        return [spin(mixed[q % 2], HC * (n_slots - q)) for q in range(PER)]

    def frame_load(s):
        return pltpu.make_async_copy(frames.at[pl.ds(s * COL_STEPS, COL_STEPS)], FS, fs_sem)

    def frame_col(h, xslot):
        return remote(FC.at[h], FR.at[xslot, 1 - h], fc_send.at[h], fc_recv.at[xslot, 1 - h], h_dev(h))

    def frame_row(v, xslot):
        src = XF.at[xslot, :, pl.ds(HR + v * (tile_h - HR), HR)]
        dst = XF.at[xslot, :, pl.ds((1 - v) * (tile_h + HR), HR)]
        return remote(src, dst, fh_send.at[v], fh_recv.at[xslot, 1 - v], v_dev(v))

    def frames_pack(xslot, t):
        for g in range(n_groups):
            rows = []
            for q in range(PER):
                r = g * PER + q
                XF[xslot, t, HR + r, :, 0:tile_w] = FS[t, r]
                rows.append(XF[xslot, t, HR + r])
            FC[0, t, g], FC[1, t, g] = pack_rows(rows, slot_x, BF)

    def frames_merge(xslot, t):
        for g in range(n_groups):
            halos = halo_rows(FR[xslot, 0, t, g], FR[xslot, 1, t, g], slot_x)
            for q in range(PER):
                r = HR + g * PER + q
                XF[xslot, t, r] = jnp.where(lane_x < tile_w, XF[xslot, t, r], halos[q])

    def frames_cols_wait(xslot, cond):
        for h in range(2):
            when_do(jnp.logical_and(cond, has_h[h]), frame_col(h, xslot).wait_send, frame_col(1 - h, xslot).wait_recv)

    def frames_rows_wait(xslot):
        for v in range(2):
            when_do(has_v[v], frame_row(v, xslot).wait_send, frame_row(1 - v, xslot).wait_recv)

    def spread(xslot, k, first, last):
        for i in range(first, last):
            store3(XB, ((k % 2) * total_rows + i) * (3 * cin), cin, XF[xslot, k, i])

    def col_copy(h, g, slot):
        return remote(CS.at[h, g], CR.at[slot, 1 - h, g], cs_send.at[h, g], cs_recv.at[slot, 1 - h, g], h_dev(h))

    def diag_copy(v, h, slot):
        return remote(DS.at[v, h], DR.at[slot, 1 - v, 1 - h], dg_send.at[v, h], dg_recv.at[slot, 1 - v, 1 - h], {**v_dev(v), **h_dev(h)})

    def row_copy(v, slot):
        return remote(RS.at[v], RR.at[slot, 1 - v], rr_send.at[v], rr_recv.at[slot, 1 - v], v_dev(v))

    wide = HR * HC
    quarter = lax.broadcasted_iota(jnp.int32, (ch * wide // LANES, LANES), 1) // wide
    parts = LANES // wide
    part_ch = ch // parts

    def col_send(g, slot, cond):
        edges = pack_rows([H[HR + g * PER + q] for q in range(PER)], slot_of, F32)
        for h in range(2):
            CS[h, g] = edges[h]
        for v in range(2):
            if g == (0 if v == 0 else n_groups - 1):
                for h in range(2):
                    first = (0 if v == 0 else PER - HR) + h * lead
                    small = jnp.zeros((part_ch, LANES), F32)
                    for c in range(parts):
                        small = jnp.where(quarter == c, spin(edges[h][c * part_ch:(c + 1) * part_ch], wide * c - HC * first), small)
                    DS[v, h] = small
        for h in range(2):
            when_do(jnp.logical_and(cond, has_h[h]), col_copy(h, g, slot).start)
        for v, h, both in diag:
            if g == (0 if v == 0 else n_groups - 1):
                when_do(jnp.logical_and(cond, both), diag_copy(v, h, slot).start)

    def col_take(g, slot):
        for h in range(2):
            when_do(has_h[h], col_copy(h, g, slot).wait_send, col_copy(1 - h, g, slot).wait_recv)
        halos = halo_rows(CR[slot, 0, g], CR[slot, 1, g], slot_of)
        for q in range(PER):
            i = HR + g * PER + q
            val = jnp.where(lane < tile_w, H[i], halos[q])
            H[i] = val
            store3(HB, i * 3 * ch, ch, val.astype(BF))

    def row_send(slot, cond):
        RS[0] = H[HR:2 * HR]
        RS[1] = H[tile_h:tile_h + HR]
        for v in range(2):
            when_do(jnp.logical_and(cond, has_v[v]), row_copy(v, slot).start)

    def row_take(slot, fresh, cslot):
        for v in range(2):
            when_do(has_v[v], row_copy(v, slot).wait_send, row_copy(1 - v, slot).wait_recv)
        if fresh:
            for v, h, cond in diag:
                when_do(cond, diag_copy(v, h, cslot).wait_send, diag_copy(1 - v, 1 - h, cslot).wait_recv)
        for v in range(2):
            for i in range(HR):
                at = i + v * (tile_h + HR)
                val = RR[slot, v, i]
                if fresh:
                    sides = []
                    for h, to in ((0, LANES - HC), (1, tile_w)):
                        small = DR[cslot, v, h]
                        sides.append(jnp.concatenate([spin(small, to - wide * c - HC * i) for c in range(parts)], axis=0))
                    val = jnp.where(lane < tile_w, val, jnp.where(lane < middle, sides[1], sides[0]))
                H[at] = val
                store3(HB, at * 3 * ch, ch, val.astype(BF))

    def frame_rows(k, i, count):
        return XB[pl.ds(((k % 2) * total_rows + i) * (3 * cin), count * 3 * cin), :]

    def zr_rows(k, first, last):
        for r in range(first, last, 2):
            i = HR + r
            cols = []
            for d in range(2):
                hb = HB[pl.ds((i + d - 1) * (3 * ch), 9 * ch), :]
                cols.append(jnp.concatenate([hb, frame_rows(k, i + d - 1, 3), ones[:48]], axis=0))
            acc = jnp.dot(WZR[...], jnp.concatenate(cols, axis=1), preferred_element_type=F32)
            gates = jnp.tanh(acc)
            for d in range(2):
                Z[i + d] = gates[:ch, d * LANES:(d + 1) * LANES]
                reset = 0.5 * gates[ch:, d * LANES:(d + 1) * LANES] + 0.5
                store3(RB, (i + d) * (3 * ch), ch, (reset * H[i + d]).astype(BF))

    def n_rows_of(t, k, first, last, keep):
        for r in range(first, last, 4):
            i = HR + r
            cols = []
            for p in range(2):
                y = i + 2 * p - 1
                cols.append(jnp.concatenate([RB[pl.ds(y * (3 * ch), 12 * ch), :], frame_rows(k, y, 4), ones], axis=0))
            acc = jnp.dot(WN[...], jnp.concatenate(cols, axis=1), preferred_element_type=F32)
            cand = jnp.tanh(acc)
            for p in range(2):
                for dy in range(2):
                    at = i + 2 * p + dy
                    inside = HR <= at < HR + tile_h
                    cand_row = cand[dy * ch:(dy + 1) * ch, p * LANES:(p + 1) * LANES]
                    update = 0.5 * Z[at] + 0.5
                    new = cand_row + update * (H[at] - cand_row)
                    mask = lane_ok if inside else lane_ok * (ok[0] if at < HR else ok[1])
                    new = jnp.where(mask != 0, new, 0.0)
                    H[at] = new
                    new_bf = new.astype(BF)
                    if keep:
                        store3(HB, at * (3 * ch), ch, new_bf)
                    if inside:
                        out[t, at - HR] = new_bf[:, :tile_w]

    def prepare_weights():
        def split3(val):
            top = float(jnp.finfo(BF).max)
            parts3 = []
            for _ in range(3):
                part = jnp.clip(val, -top, top).astype(BF).astype(F32)
                parts3.append(part)
                val = val - part
            return parts3

        def bias_rows(vals, count):
            at = lax.broadcasted_iota(jnp.int32, (count, LANES), 0)
            rows = jnp.zeros((count, LANES), F32)
            for n, part in enumerate(split3(vals)):
                rows = jnp.where(at == n, jnp.broadcast_to(part, (count, LANES)), rows)
            return rows

        def turn(dst):
            for c in range(dst.shape[1] // LANES):
                dst[:, c * LANES:(c + 1) * LANES] = KM[c * LANES:(c + 1) * LANES, :].T.astype(BF)

        taps, xtaps = 9 * ch, 9 * cin
        KM[0:taps] = 0.5 * w_hzr[...].astype(F32)
        KM[taps:taps + xtaps] = 0.5 * w_x[:, 0:2 * ch].astype(F32)
        KM[taps + xtaps:taps + xtaps + 48] = bias_rows(0.5 * bias[:, 0:2 * ch], 48)
        turn(WZR)

        def both(w, step):
            gap = jnp.zeros((step, ch), F32)
            return jnp.concatenate([jnp.concatenate([w, gap], axis=0), jnp.concatenate([gap, w], axis=0)], axis=1)
        KM[0:12 * ch] = both(w_hn[...].astype(F32), 3 * ch)
        KM[12 * ch:12 * ch + 12 * cin] = both(w_x[:, 2 * ch:3 * ch].astype(F32), 3 * cin)
        bias_n = bias[:, 2 * ch:3 * ch]
        KM[12 * ch + 12 * cin:12 * ch + 12 * cin + 64] = bias_rows(jnp.concatenate([bias_n, bias_n], axis=1), 64)
        turn(WN)

    frame_load(0).start()
    h_load = pltpu.make_async_copy(h0, HI, hi_sem)
    h_load.start()
    for s in range(2):
        for side in range(2):
            CR[s, side] = jnp.zeros(CR.shape[2:], F32)
            DR[s, side] = jnp.zeros(DR.shape[2:], F32)
            RR[s, side] = jnp.zeros(RR.shape[2:], F32)
            FR[s, side] = jnp.zeros(FR.shape[2:], BF)
            for k in range(COL_STEPS):
                XF[s, k, pl.ds(side * (tile_h + HR), HR)] = jnp.zeros((HR, cin, LANES), BF)

    barrier = pltpu.get_barrier_semaphore()
    peers = [(has_v[v], v_dev(v)) for v in range(2)] + [(has_h[h], h_dev(h)) for h in range(2)]
    peers += [(cond, {**v_dev(v), **h_dev(h)}) for v, h, cond in diag]
    for cond, dev in peers:
        @pl.when(cond)
        def _(dev=dev):
            pl.semaphore_signal(barrier, inc=1, device_id=dev, device_id_type=MESH)
    h_load.wait()

    def init_row(i, _):
        H[i] = jnp.zeros((ch, LANES), F32)
        H[i, :, 0:tile_w] = HI[i - HR]
        return 0
    lax.fori_loop(HR, HR + tile_h, init_row, 0)
    frame_load(0).wait()
    for t in range(COL_STEPS):
        frames_pack(0, t)
    frame_load(1).start()
    pl.semaphore_wait(barrier, sum(jnp.where(cond, 1, 0) for cond, _ in peers))
    for h in range(2):
        when_do(has_h[h], frame_col(h, 0).start)
    row_send(0, True)
    for g in range(n_groups):
        col_send(g, 0, True)
    prepare_weights()
    frames_cols_wait(0, True)
    for t in range(COL_STEPS):
        frames_merge(0, t)
    for v in range(2):
        when_do(has_v[v], frame_row(v, 0).start)
    spread(0, 0, HR, HR + tile_h)

    cuts = [PER * g - 1 if g else 1 for g in range(n_groups)] + [tile_h - 1]
    far = total_rows

    def super_block(s, _):
        xslot = lax.rem(s, 2)
        more = s + 1 < n_supers
        for bi in range(per_super):
            k = bi * ROW_STEPS
            t = s * COL_STEPS + k
            fresh = bi == 0
            ends = bi == per_super - 1
            if fresh:
                for g in range(n_groups):
                    col_take(g, xslot)
                    zr_rows(k, cuts[g], cuts[g + 1])
                frames_rows_wait(xslot)
                spread(xslot, 0, 0, HR)
                spread(xslot, 0, HR + tile_h, far)
            else:
                frames_cols_wait(1 - xslot, more)
                zr_rows(k, 1, tile_h - 1)
                for u in range(COL_STEPS):
                    frames_merge(1 - xslot, u)
                for v in range(2):
                    when_do(jnp.logical_and(more, has_v[v]), frame_row(v, 1 - xslot).start)
            row_take(bi % 2, fresh, xslot)
            zr_rows(k, -3, 1)
            zr_rows(k, tile_h - 1, tile_h + 3)
            n_rows_of(t, k, -2, tile_h + 2, True)
            spread(xslot, k + 1, 0, far)
            zr_rows(k + 1, -1, 5)
            zr_rows(k + 1, tile_h - 5, tile_h + 1)
            n_rows_of(t + 1, k + 1, 0, 4, not ends)
            n_rows_of(t + 1, k + 1, tile_h - 4, tile_h, not ends)
            if fresh:
                when_do(more, frame_load(s + 1).wait)
            row_send((bi + 1) % 2, more if ends else True)
            zr_rows(k + 1, 5, tile_h - 5)
            if fresh:
                for u in range(COL_STEPS):
                    frames_pack(1 - xslot, u)
            if ends:
                for g in range(n_groups):
                    n_rows_of(t + 1, k + 1, max(PER * g, 4), min(PER * (g + 1), tile_h - 4), False)
                    col_send(g, 1 - xslot, more)
                spread(1 - xslot, 0, HR, HR + tile_h)
            else:
                n_rows_of(t + 1, k + 1, 4, tile_h - 4, True)
                spread(xslot, k + 2, 0, far)
            if fresh:
                for h in range(2):
                    when_do(jnp.logical_and(more, has_h[h]), frame_col(h, 1 - xslot).start)
                when_do(s + 2 < n_supers, frame_load(s + 2).start)
        return 0
    lax.fori_loop(0, n_supers, super_block, 0)

    def last_row(i, _):
        hlast[i] = H[HR + i][:, :tile_w]
        return 0
    lax.fori_loop(0, tile_h, last_row, 0)


def solution(mesh):
    n_rows = mesh.shape['rows']
    n_cols = mesh.shape['cols']
    frame_spec = P(None, 'batch', 'rows', 'cols', None)
    state_spec = P('batch', 'rows', 'cols', None)

    def local_fn(frames, h_init, w_x, w_hzr, w_hn, gate_bias):
        steps, _, tile_h, tile_w, cin = frames.shape
        ch = h_init.shape[-1]
        total_rows = tile_h + 2 * HR
        groups = tile_h // PER
        vmem = pl.BlockSpec(memory_space=pltpu.VMEM)
        hbm = pl.BlockSpec(memory_space=pltpu.HBM)
        dma = pltpu.SemaphoreType.DMA
        corner = (ch * HR * HC // LANES, LANES)
        seq, last = pl.pallas_call(
            functools.partial(kernel, n_rows, n_cols),
            out_shape=(jax.ShapeDtypeStruct((steps, tile_h, ch, tile_w), BF),
                       jax.ShapeDtypeStruct((tile_h, ch, tile_w), F32)),
            in_specs=[hbm, hbm, vmem, vmem, vmem, vmem],
            out_specs=(vmem, vmem),
            scratch_shapes=[
                pltpu.VMEM((total_rows, ch, LANES), F32),
                pltpu.VMEM((total_rows * 3 * ch, LANES), BF),
                pltpu.VMEM((total_rows * 3 * ch, LANES), BF),
                pltpu.VMEM((2 * total_rows * 3 * cin, LANES), BF),
                pltpu.VMEM((total_rows, ch, LANES), F32),
                pltpu.VMEM((12 * ch + 12 * cin + 64, LANES), F32),
                pltpu.VMEM((2 * ch, 9 * ch + 9 * cin + 48), BF),
                pltpu.VMEM((2 * ch, 12 * ch + 12 * cin + 64), BF),
                pltpu.VMEM((tile_h, ch, tile_w), F32),
                pltpu.VMEM((COL_STEPS, tile_h, cin, tile_w), BF),
                pltpu.VMEM((2, COL_STEPS, total_rows, cin, LANES), BF),
                pltpu.VMEM((2, COL_STEPS, groups, cin, LANES), BF),
                pltpu.VMEM((2, 2, COL_STEPS, groups, cin, LANES), BF),
                pltpu.VMEM((2, groups, ch, LANES), F32),
                pltpu.VMEM((2, 2, groups, ch, LANES), F32),
                pltpu.VMEM((2, 2) + corner, F32),
                pltpu.VMEM((2, 2, 2) + corner, F32),
                pltpu.VMEM((2, HR, ch, LANES), F32),
                pltpu.VMEM((2, 2, HR, ch, LANES), F32),
                dma(()), dma(()), dma((2,)), dma((2, 2)), dma((2,)), dma((2, 2)),
                dma((2, groups)), dma((2, 2, groups)), dma((2, 2)), dma((2, 2, 2)), dma((2,)), dma((2, 2)),
            ],
            compiler_params=pltpu.CompilerParams(collective_id=0, has_side_effects=True, vmem_limit_bytes=VMEM_MIB * 1024 * 1024),
        )(frames[:, 0].transpose(0, 1, 3, 2), h_init[0].transpose(0, 2, 1), w_x.reshape(9 * cin, 3 * ch),
          w_hzr.reshape(9 * ch, 2 * ch), w_hn.reshape(9 * ch, ch), gate_bias[None])
        return seq.transpose(0, 1, 3, 2)[:, None], last.transpose(0, 2, 1)[None]

    return jax.shard_map(local_fn, mesh=mesh, in_specs=(frame_spec, state_spec, P(), P(), P(), P()), out_specs=(frame_spec, state_spec), check_vma=False)
```

profile of v0, /device:TPU:97, one launch (start us, length us, event | category | flops | bytes accessed | tf_op | source)
XLA Modules:
  0.0 142.1 jit_solution(13131998614420602519)
XLA Ops:
  0.6 0.0 copy-start
  0.6 2.3 %copy-done = bf16[24,1,48,96,16]{3,4,2,1,0:T(8,128)(2,1)S(1)} copy-done((bf16[24,1,48,96,16]{3,4,2,1,0:T(8,128)(2,1)S(1)}, bf16[24,1,48,96,16]{3,4,2,1,0:T(8,128)(2,1)}, u32[]{:S(2)}) %copy-start) | copy-done | bytes 3538968
  3.0 0.0 copy-start.1
  3.0 1.4 copy-done.1
  4.4 0.0 copy-start.2
  4.4 0.9 copy-done.2
  5.3 0.0 copy-start.3
  5.3 0.9 copy-done.3
  6.2 0.0 copy-start.4
  6.2 0.9 copy-done.4
  7.1 0.0 copy-start.5
  7.1 0.7 copy-done.5
  7.8 126.4 %shard_map.77 = (bf16[24,48,64,96]{3,2,1,0:T(8,128)(2,1)S(1)}, f32[48,64,96]{2,1,0:T(8,128)S(1)}) custom-call(bf16[24,48,16,96]{3,2,1,0:T(8,128)(2,1)S(1)} %bitcast.19, f32[48,64,96]{2,1,0:T(8,128)S(1)} %bitcast.21, bf16[144,192]{1,0:T(8,128)(2,1)S(1)} %bitcast.24, bf16[576,128]{1,0:T(8,128)(2,1)S(1)} %bitcast.22, bf16[576,64]{1,0:T(8,128)(2,1)S(1)} %bitcast.23, ...), custom_call_target="tpu_custom_call" | custom-call | tf_op jit(solution)/shard_map/pallas_call | solution.py:395
  134.1 6.9 %copy.11 = bf16[24,1,48,96,64]{3,4,2,1,0:T(8,128)(2,1)} copy(bf16[24,1,48,96,64]{3,4,2,1,0:T(8,128)(2,1)S(1)} %bitcast.18) | data formatting | bytes 28311552
  141.0 1.1 copy.12
Async XLA Ops:
  0.6 2.3 %copy-start = (bf16[24,1,48,96,16]{3,4,2,1,0:T(8,128)(2,1)S(1)}, bf16[24,1,48,96,16]{3,4,2,1,0:T(8,128)(2,1)}, u32[]{:S(2)}) copy-start(bf16[24,1,48,96,16]{3,4,2,1,0:T(8,128)(2,1)} %param.6) | copy-start | bytes 10616836
  3.0 1.4 copy-start.1
  4.4 0.9 copy-start.2
  5.3 0.9 copy-start.3
  6.2 0.9 copy-start.4
  7.1 0.7 copy-start.5
where the time goes:
time: 142 us
  Pallas kernels  126 us (89%)
  local copies, waits for them, and re-layouts  15.1 us (11%)
    pallas_call x1, Pallas kernels, local_fn(): pl.pallas_call(functools.partial(kernel, n_rows, n_cols), out_shape=(jax....  126 us
    unnamed x14, local copies, waits for them, and re-layouts  15.1 us

commit v1 on v0

--- a/solution.py
+++ b/solution.py
@@ -16,7 +16,7 @@
 HR = 2 * ROW_STEPS
 HC = 8
 COL_STEPS = HC // 2
-VMEM_MIB = 22
+VMEM_MIB = 24
 PER = LANES // HC
 
 
@@ -31,9 +31,9 @@
     return pltpu.roll(val, shift, 1) if shift else val
 
 
-def kernel(n_rows, n_cols, frames, h0, w_x, w_hzr, w_hn, bias, out, hlast,
-           H, HB, RB, XB, Z, KM, WZR, WN, HI, FS, XF, FC, FR, CS, CR, DS, DR, RS, RR,
-           hi_sem, fs_sem, fc_send, fc_recv, fh_send, fh_recv,
+def kernel(n_rows, n_cols, frames, h0, w_x_in, w_hzr_in, w_hn_in, bias_in, out, hlast,
+           H, HB, RB, XB, Z, KM, WZR, WN, HI, w_x, w_hzr, w_hn, bias, FS, XF, FC, FR, CS, CR, DS, DR, RS, RR,
+           hi_sem, w_sem, fs_sem, fc_send, fc_recv, fh_send, fh_recv,
            cs_send, cs_recv, dg_send, dg_recv, rr_send, rr_recv):
     steps, tile_h, ch, tile_w = out.shape
     cin = frames.shape[2]
@@ -82,7 +82,7 @@
         return jnp.where(even, acc[0], acc[1]), jnp.where(even, acc[1], acc[0])
 
     def halo_rows(from_left, from_right, slots):
-        turned = spin(from_left, HC * (3 - lead))
+        turned = spin(from_left, HC * (PER - 1 - n_slots - lead))
         even = slots % 2 == 0
         mixed = (jnp.where(even, from_right, turned), jnp.where(even, turned, from_right))
         return [spin(mixed[q % 2], HC * (n_slots - q)) for q in range(PER)]
@@ -274,6 +274,10 @@
     frame_load(0).start()
     h_load = pltpu.make_async_copy(h0, HI, hi_sem)
     h_load.start()
+    w_loads = [pltpu.make_async_copy(src, dst, w_sem.at[n]) for n, (src, dst) in enumerate(
+        ((w_x_in, w_x), (w_hzr_in, w_hzr), (w_hn_in, w_hn), (bias_in, bias)))]
+    for load in w_loads:
+        load.start()
     for s in range(2):
         for side in range(2):
             CR[s, side] = jnp.zeros(CR.shape[2:], F32)
@@ -307,6 +311,8 @@
     row_send(0, True)
     for g in range(n_groups):
         col_send(g, 0, True)
+    for load in w_loads:
+        load.wait()
     prepare_weights()
     frames_cols_wait(0, True)
     for t in range(COL_STEPS):
@@ -318,28 +324,54 @@
     cuts = [PER * g - 1 if g else 1 for g in range(n_groups)] + [tile_h - 1]
     far = total_rows
 
+    if COL_STEPS == 4:
+        packs, merges = {0: [0, 1], 1: [2, 3]}, {3: [0, 1, 2, 3]}
+    else:
+        packs, merges = {1: [0, 1, 2, 3], 2: [4, 5, 6, 7]}, {6: [0, 1, 2, 3], 7: [4, 5, 6, 7]}
+
     def super_block(s, _):
         xslot = lax.rem(s, 2)
         more = s + 1 < n_supers
+
+        def before(k):
+            if k == min(packs):
+                when_do(more, frame_load(s + 1).wait)
+            if k == min(merges):
+                frames_cols_wait(1 - xslot, more)
+
+        def beside(k):
+            for u in packs.get(k, []):
+                frames_pack(1 - xslot, u)
+            for u in merges.get(k, []):
+                frames_merge(1 - xslot, u)
+
+        def after(k):
+            if k == max(packs):
+                for h in range(2):
+                    when_do(jnp.logical_and(more, has_h[h]), frame_col(h, 1 - xslot).start)
+                when_do(s + 2 < n_supers, frame_load(s + 2).start)
+            if k == max(merges):
+                for v in range(2):
+                    when_do(jnp.logical_and(more, has_v[v]), frame_row(v, 1 - xslot).start)
+
         for bi in range(per_super):
             k = bi * ROW_STEPS
             t = s * COL_STEPS + k
             fresh = bi == 0
             ends = bi == per_super - 1
+            before(k)
             if fresh:
                 for g in range(n_groups):
                     col_take(g, xslot)
                     zr_rows(k, cuts[g], cuts[g + 1])
+                beside(k)
                 frames_rows_wait(xslot)
                 spread(xslot, 0, 0, HR)
                 spread(xslot, 0, HR + tile_h, far)
             else:
-                frames_cols_wait(1 - xslot, more)
                 zr_rows(k, 1, tile_h - 1)
-                for u in range(COL_STEPS):
-                    frames_merge(1 - xslot, u)
-                for v in range(2):
-                    when_do(jnp.logical_and(more, has_v[v]), frame_row(v, 1 - xslot).start)
+                beside(k)
+            after(k)
             row_take(bi % 2, fresh, xslot)
             zr_rows(k, -3, 1)
             zr_rows(k, tile_h - 1, tile_h + 3)
@@ -349,25 +381,20 @@
             zr_rows(k + 1, tile_h - 5, tile_h + 1)
             n_rows_of(t + 1, k + 1, 0, 4, not ends)
             n_rows_of(t + 1, k + 1, tile_h - 4, tile_h, not ends)
-            if fresh:
-                when_do(more, frame_load(s + 1).wait)
+            before(k + 1)
             row_send((bi + 1) % 2, more if ends else True)
             zr_rows(k + 1, 5, tile_h - 5)
-            if fresh:
-                for u in range(COL_STEPS):
-                    frames_pack(1 - xslot, u)
+            beside(k + 1)
+            after(k + 1)
             if ends:
                 for g in range(n_groups):
-                    n_rows_of(t + 1, k + 1, max(PER * g, 4), min(PER * (g + 1), tile_h - 4), False)
+                    a, b = max(PER * g, 4), min(PER * (g + 1), tile_h - 4)
+                    n_rows_of(t + 1, k + 1, a, b, False)
                     col_send(g, 1 - xslot, more)
                 spread(1 - xslot, 0, HR, HR + tile_h)
             else:
                 n_rows_of(t + 1, k + 1, 4, tile_h - 4, True)
                 spread(xslot, k + 2, 0, far)
-            if fresh:
-                for h in range(2):
-                    when_do(jnp.logical_and(more, has_h[h]), frame_col(h, 1 - xslot).start)
-                when_do(s + 2 < n_supers, frame_load(s + 2).start)
         return 0
     lax.fori_loop(0, n_supers, super_block, 0)
 
@@ -396,7 +423,7 @@
             functools.partial(kernel, n_rows, n_cols),
             out_shape=(jax.ShapeDtypeStruct((steps, tile_h, ch, tile_w), BF),
                        jax.ShapeDtypeStruct((tile_h, ch, tile_w), F32)),
-            in_specs=[hbm, hbm, vmem, vmem, vmem, vmem],
+            in_specs=[hbm] * 6,
             out_specs=(vmem, vmem),
             scratch_shapes=[
                 pltpu.VMEM((total_rows, ch, LANES), F32),
@@ -408,6 +435,10 @@
                 pltpu.VMEM((2 * ch, 9 * ch + 9 * cin + 48), BF),
                 pltpu.VMEM((2 * ch, 12 * ch + 12 * cin + 64), BF),
                 pltpu.VMEM((tile_h, ch, tile_w), F32),
+                pltpu.VMEM((9 * cin, 3 * ch), BF),
+                pltpu.VMEM((9 * ch, 2 * ch), BF),
+                pltpu.VMEM((9 * ch, ch), BF),
+                pltpu.VMEM((1, 3 * ch), F32),
                 pltpu.VMEM((COL_STEPS, tile_h, cin, tile_w), BF),
                 pltpu.VMEM((2, COL_STEPS, total_rows, cin, LANES), BF),
                 pltpu.VMEM((2, COL_STEPS, groups, cin, LANES), BF),
@@ -418,12 +449,13 @@
                 pltpu.VMEM((2, 2, 2) + corner, F32),
                 pltpu.VMEM((2, HR, ch, LANES), F32),
                 pltpu.VMEM((2, 2, HR, ch, LANES), F32),
-                dma(()), dma(()), dma((2,)), dma((2, 2)), dma((2,)), dma((2, 2)),
+                dma(()), dma((4,)), dma(()), dma((2,)), dma((2, 2)), dma((2,)), dma((2, 2)),
                 dma((2, groups)), dma((2, 2, groups)), dma((2, 2)), dma((2, 2, 2)), dma((2,)), dma((2, 2)),
             ],
             compiler_params=pltpu.CompilerParams(collective_id=0, has_side_effects=True, vmem_limit_bytes=VMEM_MIB * 1024 * 1024),
-        )(frames[:, 0].transpose(0, 1, 3, 2), h_init[0].transpose(0, 2, 1), w_x.reshape(9 * cin, 3 * ch),
-          w_hzr.reshape(9 * ch, 2 * ch), w_hn.reshape(9 * ch, ch), gate_bias[None])
+        )(*[pltpu.with_memory_space_constraint(a, pltpu.HBM) for a in (
+            frames[:, 0].transpose(0, 1, 3, 2), h_init[0].transpose(0, 2, 1), w_x.reshape(9 * cin, 3 * ch),
+            w_hzr.reshape(9 * ch, 2 * ch), w_hn.reshape(9 * ch, ch), gate_bias[None])])
         return seq.transpose(0, 1, 3, 2)[:, None], last.transpose(0, 2, 1)[None]
 
     return jax.shard_map(local_fn, mesh=mesh, in_specs=(frame_spec, state_spec, P(), P(), P(), P()), out_specs=(frame_spec, state_spec), check_vma=False)

time: 142 us -> 125 us (0.88)
  Pallas kernels: 126 us -> 116 us
  local copies, waits for them, and re-layouts: 15.1 us -> 8 us
    pallas_call x1, Pallas kernels: 126 us -> 116 us  [local_fn(): pl.pallas_call(functools.partial(kernel, n_rows, n_cols), out_shape=(jax....]
    unnamed x14 -> x2, local copies, waits for them, and re-layouts: 15.1 us -> 8 us
where the time goes in v1:
time: 125 us
  Pallas kernels  116 us (93%)
  local copies, waits for them, and re-layouts  8 us (6%)
    pallas_call x1, Pallas kernels, local_fn(): pl.pallas_call(functools.partial(kernel, n_rows, n_cols), out_shape=(jax....  116 us
    unnamed x2, local copies, waits for them, and re-layouts  8 us

profile of v1, /device:TPU:97, one launch (start us, length us, event | category | flops | bytes accessed | tf_op | source)
XLA Modules:
  0.0 124.6 jit_solution(3442106764081622229)
XLA Ops:
  0.6 116.0 %shard_map.77 = (bf16[24,48,64,96]{3,2,1,0:T(8,128)(2,1)S(1)}, f32[48,64,96]{2,1,0:T(8,128)S(1)}) custom-call(bf16[24,48,16,96]{3,2,1,0:T(8,128)(2,1)} %bitcast.20, f32[48,64,96]{2,1,0:T(8,128)} %bitcast.21, bf16[144,192]{1,0:T(8,128)(2,1)} %bitcast.24, bf16[576,128]{1,0:T(8,128)(2,1)} %bitcast.22, bf16[576,64]{1,0:T(8,128)(2,1)} %bitcast.23, f32[1,192]{1,0:T(1,128)} %bitcast.25), custom_call_target="tpu_custom_call" | custom-call | tf_op jit(solution)/shard_map/pallas_call | solution.py:422
  116.6 6.9 %copy.11 = bf16[24,1,48,96,64]{3,4,2,1,0:T(8,128)(2,1)} copy(bf16[24,1,48,96,64]{3,4,2,1,0:T(8,128)(2,1)S(1)} %bitcast.18) | data formatting | bytes 28311552
  123.4 1.1 copy.12

commit v2 on v1

--- a/solution.py
+++ b/solution.py
@@ -21,9 +21,9 @@
 
 
 def store3(buf, base, size, val):
-    buf[pl.ds(base, size), :] = pltpu.roll(val, 1, 1)
-    buf[pl.ds(base + size, size), :] = val
-    buf[pl.ds(base + 2 * size, size), :] = pltpu.roll(val, LANES - 1, 1)
+    buf[pl.ds(base, size), :] = pltpu.roll(val, 1, 1).astype(BF)
+    buf[pl.ds(base + size, size), :] = val.astype(BF)
+    buf[pl.ds(base + 2 * size, size), :] = pltpu.roll(val, LANES - 1, 1).astype(BF)
 
 
 def spin(val, shift):
@@ -73,11 +73,13 @@
     lane_ok = jnp.where(lane < tile_w, 1, jnp.where(lane < tile_w + HC, ok[3], jnp.where(lane >= LANES - HC, ok[2], 0)))
     lead = n_slots - 1
 
-    def pack_rows(rows, slots, dtype):
+    def strip_masks(slots):
+        return [jnp.logical_or(slots == q, slots == (lead + q) % PER) for q in range(PER)]
+
+    def pack_rows(rows, slots, dtype, masks):
         acc = [jnp.zeros(rows[0].shape, dtype), jnp.zeros(rows[0].shape, dtype)]
         for q, val in enumerate(rows):
-            here = jnp.logical_or(slots == q, slots == (lead + q) % PER)
-            acc[q % 2] = jnp.where(here, spin(val, HC * q), acc[q % 2])
+            acc[q % 2] = jnp.where(masks[q], spin(val, HC * q), acc[q % 2])
         even = slots % 2 == 0
         return jnp.where(even, acc[0], acc[1]), jnp.where(even, acc[1], acc[0])
 
@@ -99,20 +101,22 @@
         return remote(src, dst, fh_send.at[v], fh_recv.at[xslot, 1 - v], v_dev(v))
 
     def frames_pack(xslot, t):
+        masks = strip_masks(slot_x)
         for g in range(n_groups):
             rows = []
             for q in range(PER):
                 r = g * PER + q
                 XF[xslot, t, HR + r, :, 0:tile_w] = FS[t, r]
                 rows.append(XF[xslot, t, HR + r])
-            FC[0, t, g], FC[1, t, g] = pack_rows(rows, slot_x, BF)
+            FC[0, t, g], FC[1, t, g] = pack_rows(rows, slot_x, BF, masks)
 
     def frames_merge(xslot, t):
+        own = lane_x < tile_w
         for g in range(n_groups):
             halos = halo_rows(FR[xslot, 0, t, g], FR[xslot, 1, t, g], slot_x)
             for q in range(PER):
                 r = HR + g * PER + q
-                XF[xslot, t, r] = jnp.where(lane_x < tile_w, XF[xslot, t, r], halos[q])
+                XF[xslot, t, r] = jnp.where(own, XF[xslot, t, r], halos[q])
 
     def frames_cols_wait(xslot, cond):
         for h in range(2):
@@ -141,7 +145,7 @@
     part_ch = ch // parts
 
     def col_send(g, slot, cond):
-        edges = pack_rows([H[HR + g * PER + q] for q in range(PER)], slot_of, F32)
+        edges = pack_rows([H[HR + g * PER + q] for q in range(PER)], slot_of, F32, strip_masks(slot_of))
         for h in range(2):
             CS[h, g] = edges[h]
         for v in range(2):
@@ -162,11 +166,12 @@
         for h in range(2):
             when_do(has_h[h], col_copy(h, g, slot).wait_send, col_copy(1 - h, g, slot).wait_recv)
         halos = halo_rows(CR[slot, 0, g], CR[slot, 1, g], slot_of)
+        own = lane < tile_w
         for q in range(PER):
             i = HR + g * PER + q
-            val = jnp.where(lane < tile_w, H[i], halos[q])
+            val = jnp.where(own, H[i], halos[q])
             H[i] = val
-            store3(HB, i * 3 * ch, ch, val.astype(BF))
+            store3(HB, i * 3 * ch, ch, val)
 
     def row_send(slot, cond):
         RS[0] = H[HR:2 * HR]
@@ -191,26 +196,28 @@
                         sides.append(jnp.concatenate([spin(small, to - wide * c - HC * i) for c in range(parts)], axis=0))
                     val = jnp.where(lane < tile_w, val, jnp.where(lane < middle, sides[1], sides[0]))
                 H[at] = val
-                store3(HB, at * 3 * ch, ch, val.astype(BF))
+                store3(HB, at * 3 * ch, ch, val)
 
     def frame_rows(k, i, count):
         return XB[pl.ds(((k % 2) * total_rows + i) * (3 * cin), count * 3 * cin), :]
 
     def zr_rows(k, first, last):
+        ones_zr = ones[:48]
         for r in range(first, last, 2):
             i = HR + r
             cols = []
             for d in range(2):
                 hb = HB[pl.ds((i + d - 1) * (3 * ch), 9 * ch), :]
-                cols.append(jnp.concatenate([hb, frame_rows(k, i + d - 1, 3), ones[:48]], axis=0))
+                cols.append(jnp.concatenate([hb, frame_rows(k, i + d - 1, 3), ones_zr], axis=0))
             acc = jnp.dot(WZR[...], jnp.concatenate(cols, axis=1), preferred_element_type=F32)
             gates = jnp.tanh(acc)
             for d in range(2):
                 Z[i + d] = gates[:ch, d * LANES:(d + 1) * LANES]
                 reset = 0.5 * gates[ch:, d * LANES:(d + 1) * LANES] + 0.5
-                store3(RB, (i + d) * (3 * ch), ch, (reset * H[i + d]).astype(BF))
+                store3(RB, (i + d) * (3 * ch), ch, reset * H[i + d])
 
     def n_rows_of(t, k, first, last, keep):
+        keep_in = lane_ok != 0
         for r in range(first, last, 4):
             i = HR + r
             cols = []
@@ -226,12 +233,12 @@
                     cand_row = cand[dy * ch:(dy + 1) * ch, p * LANES:(p + 1) * LANES]
                     update = 0.5 * Z[at] + 0.5
                     new = cand_row + update * (H[at] - cand_row)
-                    mask = lane_ok if inside else lane_ok * (ok[0] if at < HR else ok[1])
-                    new = jnp.where(mask != 0, new, 0.0)
+                    mask = keep_in if inside else lane_ok * (ok[0] if at < HR else ok[1]) != 0
+                    new = jnp.where(mask, new, 0.0)
                     H[at] = new
                     new_bf = new.astype(BF)
                     if keep:
-                        store3(HB, at * (3 * ch), ch, new_bf)
+                        store3(HB, at * (3 * ch), ch, new)
                     if inside:
                         out[t, at - HR] = new_bf[:, :tile_w]
 
@@ -372,10 +379,16 @@
                 zr_rows(k, 1, tile_h - 1)
                 beside(k)
             after(k)
+            if not fresh:
+                n_rows_of(t, k, 2, tile_h - 2, True)
             row_take(bi % 2, fresh, xslot)
             zr_rows(k, -3, 1)
             zr_rows(k, tile_h - 1, tile_h + 3)
-            n_rows_of(t, k, -2, tile_h + 2, True)
+            if fresh:
+                n_rows_of(t, k, -2, tile_h + 2, True)
+            else:
+                n_rows_of(t, k, -2, 2, True)
+                n_rows_of(t, k, tile_h - 2, tile_h + 2, True)
             spread(xslot, k + 1, 0, far)
             zr_rows(k + 1, -1, 5)
             zr_rows(k + 1, tile_h - 5, tile_h + 1)
@@ -383,12 +396,15 @@
             n_rows_of(t + 1, k + 1, tile_h - 4, tile_h, not ends)
             before(k + 1)
             row_send((bi + 1) % 2, more if ends else True)
-            zr_rows(k + 1, 5, tile_h - 5)
+            late = PER * (n_groups - 1) + 1 if ends else tile_h - 5
+            zr_rows(k + 1, 5, late)
             beside(k + 1)
             after(k + 1)
             if ends:
                 for g in range(n_groups):
                     a, b = max(PER * g, 4), min(PER * (g + 1), tile_h - 4)
+                    if g == 1:
+                        zr_rows(k + 1, late, tile_h - 5)
                     n_rows_of(t + 1, k + 1, a, b, False)
                     col_send(g, 1 - xslot, more)
                 spread(1 - xslot, 0, HR, HR + tile_h)

time: 125 us -> 121 us (0.968)
  Pallas kernels: 116 us -> 112 us
    pallas_call x1, Pallas kernels: 116 us -> 112 us  [local_fn(): pl.pallas_call(functools.partial(kernel, n_rows, n_cols), out_shape=(jax....]
where the time goes in v2:
time: 121 us
  Pallas kernels  112 us (93%)
  local copies, waits for them, and re-layouts  8 us (7%)
    pallas_call x1, Pallas kernels, local_fn(): pl.pallas_call(functools.partial(kernel, n_rows, n_cols), out_shape=(jax....  112 us
    unnamed x2, local copies, waits for them, and re-layouts  8 us

profile of v2, /device:TPU:97, one launch (start us, length us, event | category | flops | bytes accessed | tf_op | source)
XLA Modules:
  0.0 120.7 jit_solution(5451709518056453676)
XLA Ops:
  0.6 112.1 %shard_map.77 = (bf16[24,48,64,96]{3,2,1,0:T(8,128)(2,1)S(1)}, f32[48,64,96]{2,1,0:T(8,128)S(1)}) custom-call(bf16[24,48,16,96]{3,2,1,0:T(8,128)(2,1)} %bitcast.20, f32[48,64,96]{2,1,0:T(8,128)} %bitcast.21, bf16[144,192]{1,0:T(8,128)(2,1)} %bitcast.24, bf16[576,128]{1,0:T(8,128)(2,1)} %bitcast.22, bf16[576,64]{1,0:T(8,128)(2,1)} %bitcast.23, f32[1,192]{1,0:T(1,128)} %bitcast.25), custom_call_target="tpu_custom_call" | custom-call | tf_op jit(solution)/shard_map/pallas_call | solution.py:438
  112.7 6.9 %copy.11 = bf16[24,1,48,96,64]{3,4,2,1,0:T(8,128)(2,1)} copy(bf16[24,1,48,96,64]{3,4,2,1,0:T(8,128)(2,1)S(1)} %bitcast.18) | data formatting | bytes 28311552
  119.6 1.1 copy.12

commit v3 on v2

--- a/solution.py
+++ b/solution.py
@@ -148,6 +148,8 @@
         edges = pack_rows([H[HR + g * PER + q] for q in range(PER)], slot_of, F32, strip_masks(slot_of))
         for h in range(2):
             CS[h, g] = edges[h]
+        for h in range(2):
+            when_do(jnp.logical_and(cond, has_h[h]), col_copy(h, g, slot).start)
         for v in range(2):
             if g == (0 if v == 0 else n_groups - 1):
                 for h in range(2):
@@ -156,8 +158,6 @@
                     for c in range(parts):
                         small = jnp.where(quarter == c, spin(edges[h][c * part_ch:(c + 1) * part_ch], wide * c - HC * first), small)
                     DS[v, h] = small
-        for h in range(2):
-            when_do(jnp.logical_and(cond, has_h[h]), col_copy(h, g, slot).start)
         for v, h, both in diag:
             if g == (0 if v == 0 else n_groups - 1):
                 when_do(jnp.logical_and(cond, both), diag_copy(v, h, slot).start)

time: 121 us -> 120 us (level)
  no operation moved by 1% of the time
where the time goes in v3:
time: 120 us
  Pallas kernels  111 us (92%)
  local copies, waits for them, and re-layouts  8 us (7%)
    pallas_call x1, Pallas kernels, local_fn(): pl.pallas_call(functools.partial(kernel, n_rows, n_cols), out_shape=(jax....  111 us
    unnamed x2, local copies, waits for them, and re-layouts  8 us

profile of v3, /device:TPU:97, one launch (start us, length us, event | category | flops | bytes accessed | tf_op | source)
XLA Modules:
  0.0 120.1 jit_solution(633899546576540038)
XLA Ops:
  0.6 111.5 %shard_map.77 = (bf16[24,48,64,96]{3,2,1,0:T(8,128)(2,1)S(1)}, f32[48,64,96]{2,1,0:T(8,128)S(1)}) custom-call(bf16[24,48,16,96]{3,2,1,0:T(8,128)(2,1)} %bitcast.20, f32[48,64,96]{2,1,0:T(8,128)} %bitcast.21, bf16[144,192]{1,0:T(8,128)(2,1)} %bitcast.24, bf16[576,128]{1,0:T(8,128)(2,1)} %bitcast.22, bf16[576,64]{1,0:T(8,128)(2,1)} %bitcast.23, f32[1,192]{1,0:T(1,128)} %bitcast.25), custom_call_target="tpu_custom_call" | custom-call | tf_op jit(solution)/shard_map/pallas_call | solution.py:438
  112.1 6.9 %copy.11 = bf16[24,1,48,96,64]{3,4,2,1,0:T(8,128)(2,1)} copy(bf16[24,1,48,96,64]{3,4,2,1,0:T(8,128)(2,1)S(1)} %bitcast.18) | data formatting | bytes 28311552
  119.0 1.1 copy.12
